TPU v7x, 128 devices: a whole 4x4x4 slice. The times are simulated.
128 devices in a mesh: data: 32 (over z, y, x_hi), width: 4 (over x_lo, core).
Axes of the slice: x: 4 (x_hi: 2, x_lo: 2; x = x_hi * 2 + x_lo), y: 4, z: 4, core: 2. Of those that a mesh axis runs over, the one named last changes fastest.
Arguments:
- grad_up: float32 [32, 768, 3072], P('data', None, 'width'), may hold values from -6 to 6
- grad_down: float32 [32, 3072, 768], P('data', 'width'), may hold values from -6 to 6
- grad_query: float32 [32, 768, 768], P('data', None, 'width'), may hold values from -6 to 6
- grad_key: float32 [32, 768, 768], P('data', None, 'width'), may hold values from -6 to 6
- grad_value: float32 [32, 768, 768], P('data', None, 'width'), may hold values from -6 to 6
- grad_mixed: float32 [32, 768, 768], P('data', 'width'), may hold values from -6 to 6
- grad_norm: float32 [32, 768], P('data'), may hold values from -12 to 12
- weight_up: float32 [768, 3072], P('data', 'width'), may hold values from -0.21875 to 0.21875
- weight_down: float32 [3072, 768], P('width', 'data'), may hold values from -0.109375 to 0.109375
- weight_query: float32 [768, 768], P('data', 'width'), may hold values from -0.21875 to 0.21875
- weight_key: float32 [768, 768], P('data', 'width'), may hold values from -0.21875 to 0.21875
- weight_value: float32 [768, 768], P('data', 'width'), may hold values from -0.21875 to 0.21875
- weight_mixed: float32 [768, 768], P('width', 'data'), may hold values from -0.21875 to 0.21875
- weight_norm: float32 [768], P('data'), may hold values from 0.25 to 1.75
- moment_up: float32 [768, 3072], P('data', 'width'), may hold values from 0.05 to 0.8
- moment_down: float32 [3072, 768], P('width', 'data'), may hold values from 0.05 to 0.8
- moment_query: float32 [768, 768], P('data', 'width'), may hold values from 0.05 to 0.8
- moment_key: float32 [768, 768], P('data', 'width'), may hold values from 0.05 to 0.8
- moment_value: float32 [768, 768], P('data', 'width'), may hold values from 0.05 to 0.8
- moment_mixed: float32 [768, 768], P('width', 'data'), may hold values from 0.05 to 0.8
- moment_norm: float32 [768], P('data'), may hold values from 0.05 to 0.8
Outputs:
- copy_up: bfloat16 [768, 3072], P(None, 'width')
- copy_down: bfloat16 [3072, 768], P('width')
- copy_query: bfloat16 [768, 768], P(None, 'width')
- copy_key: bfloat16 [768, 768], P(None, 'width')
- copy_value: bfloat16 [768, 768], P(None, 'width')
- copy_mixed: bfloat16 [768, 768], P('width')
- copy_norm: bfloat16 [768], replicated
- new_up: float32 [768, 3072], P('data', 'width')
- new_down: float32 [3072, 768], P('width', 'data')
- new_query: float32 [768, 768], P('data', 'width')
- new_key: float32 [768, 768], P('data', 'width')
- new_value: float32 [768, 768], P('data', 'width')
- new_mixed: float32 [768, 768], P('width', 'data')
- new_norm: float32 [768], P('data')
- state_new_up: float32 [768, 3072], P('data', 'width')
- state_new_down: float32 [3072, 768], P('width', 'data')
- state_new_query: float32 [768, 768], P('data', 'width')
- state_new_key: float32 [768, 768], P('data', 'width')
- state_new_value: float32 [768, 768], P('data', 'width')
- state_new_mixed: float32 [768, 768], P('width', 'data')
- state_new_norm: float32 [768], P('data')
All inputs are finite; a program needn't handle non-finite values.
Results may differ from a plain program's by a relative error of at most 0.0004.
Values may be sent and summed in bfloat16 or wider, within the bound.
A program may use at most 128 MiB of HBM per device.

v0:
```python
import jax
import jax.numpy as jnp
from jax import lax
from jax.sharding import PartitionSpec as P

learn_rate = 0.05
hold_rate = 0.9


def in_blocks(x, dim, devices):
    shape = x.shape
    blocks = x.reshape(*shape[:dim], devices, shape[dim] // devices, *shape[dim + 1 :])
    return jnp.moveaxis(blocks, dim, 0)


def one_scatter(arrays, axis, dims):
    devices = lax.axis_size(axis)
    blocks = [in_blocks(a, dim, devices) for a, dim in zip(arrays, dims)]
    lines = jnp.concatenate([b.reshape(devices, -1) for b in blocks], axis=1)
    span = max(16, -(-lines.shape[1] // 1024) * 8)
    lines = jnp.pad(lines, ((0, 0), (0, span * 128 - lines.shape[1]))).reshape(-1, 128)
    line, at, gathered = (lax.psum_scatter(lines, axis, tiled=True).reshape(-1), 0, [])
    for b in blocks:
        part = b[0]
        gathered.append(line[at : at + part.size].reshape(part.shape))
        at += part.size
    return tuple(gathered)


def turned_gather(arrays, axis, dims):
    turned = [jnp.moveaxis(a, dim, 0) for a, dim in zip(arrays, dims)]
    widths = [t[0].size for t in turned]
    both = jnp.concatenate([t.reshape(-1, w) for t, w in zip(turned, widths)], axis=1)
    whole = lax.all_gather(both, axis, axis=0, tiled=True)
    blocks = jnp.split(whole, [sum(widths[:k]) for k in range(1, len(widths))], axis=1)
    return tuple(
        (
            jnp.moveaxis(b.reshape(-1, *t.shape[1:]), 0, dim)
            for b, t, dim in zip(blocks, turned, dims)
        )
    )


def on_device(
    grad_up,
    grad_down,
    grad_query,
    grad_key,
    grad_value,
    grad_mixed,
    grad_norm,
    weight_up,
    weight_down,
    weight_query,
    weight_key,
    weight_value,
    weight_mixed,
    weight_norm,
    moment_up,
    moment_down,
    moment_query,
    moment_key,
    moment_value,
    moment_mixed,
    moment_norm,
):
    mean_up, mean_down, mean_query, mean_key, mean_value, mean_mixed, mean_norm = one_scatter(
        (
            grad_up[0],
            grad_down[0],
            grad_query[0],
            grad_key[0],
            grad_value[0],
            grad_mixed[0],
            grad_norm[0],
        ),
        "data",
        (0, 1, 0, 0, 0, 1, 0),
    )
    mean_rate = lax.axis_size("data") ** (-0.5)
    mean_up = mean_up * mean_rate
    mean_down = mean_down * mean_rate
    mean_query = mean_query * mean_rate
    mean_key = mean_key * mean_rate
    mean_value = mean_value * mean_rate
    mean_mixed = mean_mixed * mean_rate
    mean_norm = mean_norm * mean_rate
    state_new_up = hold_rate * moment_up + (1.0 - hold_rate) * mean_up * mean_up
    new_up = weight_up - learn_rate * mean_up * lax.rsqrt(state_new_up + 1e-06)
    state_new_down = hold_rate * moment_down + (1.0 - hold_rate) * mean_down * mean_down
    new_down = weight_down - learn_rate * mean_down * lax.rsqrt(state_new_down + 1e-06)
    state_new_query = hold_rate * moment_query + (1.0 - hold_rate) * mean_query * mean_query
    new_query = weight_query - learn_rate * mean_query * lax.rsqrt(state_new_query + 1e-06)
    state_new_key = hold_rate * moment_key + (1.0 - hold_rate) * mean_key * mean_key
    new_key = weight_key - learn_rate * mean_key * lax.rsqrt(state_new_key + 1e-06)
    state_new_value = hold_rate * moment_value + (1.0 - hold_rate) * mean_value * mean_value
    new_value = weight_value - learn_rate * mean_value * lax.rsqrt(state_new_value + 1e-06)
    state_new_mixed = hold_rate * moment_mixed + (1.0 - hold_rate) * mean_mixed * mean_mixed
    new_mixed = weight_mixed - learn_rate * mean_mixed * lax.rsqrt(state_new_mixed + 1e-06)
    state_new_norm = hold_rate * moment_norm + (1.0 - hold_rate) * mean_norm * mean_norm
    new_norm = weight_norm - learn_rate * mean_norm * lax.rsqrt(state_new_norm + 1e-06)
    copy_up, copy_down, copy_query, copy_key, copy_value, copy_mixed, copy_norm = turned_gather(
        (
            new_up.astype(jnp.bfloat16),
            new_down.astype(jnp.bfloat16),
            new_query.astype(jnp.bfloat16),
            new_key.astype(jnp.bfloat16),
            new_value.astype(jnp.bfloat16),
            new_mixed.astype(jnp.bfloat16),
            new_norm.astype(jnp.bfloat16),
        ),
        "data",
        (0, 1, 0, 0, 0, 1, 0),
    )
    return (
        copy_up,
        copy_down,
        copy_query,
        copy_key,
        copy_value,
        copy_mixed,
        copy_norm,
        new_up,
        new_down,
        new_query,
        new_key,
        new_value,
        new_mixed,
        new_norm,
        state_new_up,
        state_new_down,
        state_new_query,
        state_new_key,
        state_new_value,
        state_new_mixed,
        state_new_norm,
    )


def solution(mesh):
    return jax.shard_map(
        on_device,
        mesh=mesh,
        in_specs=(
            P("data", None, "width"),
            P("data", "width", None),
            P("data", None, "width"),
            P("data", None, "width"),
            P("data", None, "width"),
            P("data", "width", None),
            P("data", None),
            P("data", "width"),
            P("width", "data"),
            P("data", "width"),
            P("data", "width"),
            P("data", "width"),
            P("width", "data"),
            P("data"),
            P("data", "width"),
            P("width", "data"),
            P("data", "width"),
            P("data", "width"),
            P("data", "width"),
            P("width", "data"),
            P("data"),
        ),
        out_specs=(
            P(None, "width"),
            P("width", None),
            P(None, "width"),
            P(None, "width"),
            P(None, "width"),
            P("width", None),
            P(),
            P("data", "width"),
            P("width", "data"),
            P("data", "width"),
            P("data", "width"),
            P("data", "width"),
            P("width", "data"),
            P("data"),
            P("data", "width"),
            P("width", "data"),
            P("data", "width"),
            P("data", "width"),
            P("data", "width"),
            P("width", "data"),
            P("data"),
        ),
        check_vma=False,
    )
```

profile of v0, /device:TPU:0, one launch (start us, length us, event | category | flops | bytes accessed | tf_op | source)
XLA Modules:
  0.0 577.1 jit_solution(8048873237569944627)
XLA Ops:
  7.2 2.0 copy.97
  9.3 6.6 %copy.98 = f32[32,768,24]{2,1,0:T(8,128)} copy(f32[32,768,24]{1,2,0:T(8,128)S(1)} %bitcast.19) | data formatting | bytes 4718592 | tf_op jit(solution)/shard_map/transpose | solution.py:13
  15.9 11.5 %reshape.120 = f32[32,18432]{1,0:T(8,128)} reshape(f32[32,768,24]{2,1,0:T(8,128)} %copy.98) | data formatting | bytes 4718592 | tf_op jit(solution)/shard_map/reshape | solution.py:19
  27.4 1.9 reshape_reshape_squeeze.12
  29.3 1.6 constant_dynamic-update-slice_fusion.6
  31.2 1.1 reshape_reshape_squeeze.13
  32.5 1.1 reshape_reshape_squeeze.14
  33.6 1.3 copy.101
  34.9 1.1 reshape_reshape_squeeze.15
  36.1 1.1 copy.102
  37.2 2.0 copy.103
  39.2 3.0 reshape.121
  42.3 3.3 constant_dynamic-update-slice_fusion.5
  45.6 2.0 constant_dynamic-update-slice_fusion.4
  47.6 1.9 constant_dynamic-update-slice_fusion.3
  49.6 0.9 constant_dynamic-update-slice_fusion.2
  50.4 0.9 constant_dynamic-update-slice_fusion.1
  51.9 6.4 %pad.4 = f32[32,56320]{1,0:T(8,128)} pad(f32[32,55320]{1,0:T(8,128)} %constant_dynamic-update-slice_fusion, f32[]{:T(128)} %constant.15.clone.1), padding=0_0x0_1000 | pad | bytes 14289924 | tf_op jit(solution)/shard_map/jit(_pad)/pad | solution.py:21
  58.3 6.8 %reshape.122 = f32[14080,128]{1,0:T(8,128)} reshape(f32[32,56320]{1,0:T(8,128)} %pad.4) | data formatting | bytes 14417920 | tf_op jit(solution)/shard_map/reshape | solution.py:21
  66.9 406.0 %all-reduce.4.cloned.1.call-done = f32[14080,128]{1,0:T(8,128)} async-done(((f32[14080,128]{1,0:T(8,128)}), f32[14080,128]{1,0:T(8,128)}) %all-reduce.4.cloned.1.call-update) | async-done | bytes 7208976
  473.0 0.8 multiply_multiply_fusion.2
  474.6 1.0 multiply_multiply_fusion
  476.4 1.0 dynamic-slice_bitcast_fusion
  482.1 76.9 %all-gather.2.cloned.1.call-done = bf16[768,2305]{1,0:T(8,128)(2,1)} async-done(((bf16[24,2305]{1,0:T(8,128)(2,1)}), bf16[768,2305]{1,0:T(8,128)(2,1)}) %all-gather.2.cloned.1.call-update) | async-done | bytes 3540496 | tf_op jit(solution)/shard_map/all_gather | solution.py:34
  559.0 2.8 slice_bitcast_fusion
  561.8 1.4 copy.109
  563.2 1.9 slice_bitcast_fusion.1
  565.1 0.9 copy.110
  566.0 0.9 copy.111
  566.8 0.9 copy.112
  567.7 0.9 copy.113
  568.6 1.7 slice_reduce_fusion
  (76 shorter events, 8.6 us)
Async XLA Ops:
  7.2 465.8 %all-reduce.4.cloned.1.call-start = ((), (), s32[]{:S(2)}) async-start(), calls=%async_computation.1 | async-start | bytes 14417920
  27.4 3.5 copy-start.2
  27.4 4.8 copy-start.3
  30.9 5.1 copy-start.4
  32.3 10.0 %copy-start.17 = (f32[1,768]{1,0:T(1,128)S(1)}, f32[1,768]{1,0:T(1,128)}, u32[]{:S(2)}) copy-start(f32[1,768]{1,0:T(1,128)} %param.27) | copy-start | bytes 9220
  42.2 7.3 %copy-start.1 = (f32[32,4608]{1,0:T(8,128)S(1)}, f32[32,4608]{1,0:T(8,128)}, u32[]{:S(2)}) copy-start(f32[32,4608]{1,0:T(8,128)} %reshape_reshape_squeeze.15) | copy-start | bytes 1769476
  42.2 8.2 %copy-start = (f32[32,4608]{1,0:T(8,128)S(1)}, f32[32,4608]{1,0:T(8,128)}, u32[]{:S(2)}) copy-start(f32[32,4608]{1,0:T(8,128)} %reshape.121) | copy-start | bytes 1769476
  65.0 0.7 copy-start.20
  65.0 412.3 %copy-start.18 = (f32[24]{0:T(128)S(1)}, f32[24]{0:T(128)}, u32[]{:S(2)}) copy-start(f32[24]{0:T(128)} %param.34) | copy-start | bytes 292
  65.0 412.3 %copy-start.19 = (f32[24]{0:T(128)S(1)}, f32[24]{0:T(128)}, u32[]{:S(2)}) copy-start(f32[24]{0:T(128)} %param.41) | copy-start | bytes 292
  65.0 413.0 %copy-start.9 = (f32[192,24]{0,1:T(8,128)S(1)}, f32[192,24]{0,1:T(8,128)}, u32[]{:S(2)}) copy-start(f32[192,24]{0,1:T(8,128)} %param.33) | copy-start | bytes 55300
  65.1 413.0 %copy-start.10 = (f32[192,24]{0,1:T(8,128)S(1)}, f32[192,24]{0,1:T(8,128)}, u32[]{:S(2)}) copy-start(f32[192,24]{0,1:T(8,128)} %param.40) | copy-start | bytes 55300
  65.1 413.6 %copy-start.11 = (f32[24,192]{1,0:T(8,128)S(1)}, f32[24,192]{1,0:T(8,128)}, u32[]{:S(2)}) copy-start(f32[24,192]{1,0:T(8,128)} %param.30) | copy-start | bytes 55300
  65.1 413.6 %copy-start.12 = (f32[24,192]{1,0:T(8,128)S(1)}, f32[24,192]{1,0:T(8,128)}, u32[]{:S(2)}) copy-start(f32[24,192]{1,0:T(8,128)} %param.37) | copy-start | bytes 55300
  65.1 414.2 %copy-start.5 = (f32[768,24]{0,1:T(8,128)S(1)}, f32[768,24]{0,1:T(8,128)}, u32[]{:S(2)}) copy-start(f32[768,24]{0,1:T(8,128)} %param.29) | copy-start | bytes 221188
  65.1 414.2 %copy-start.6 = (f32[768,24]{0,1:T(8,128)S(1)}, f32[768,24]{0,1:T(8,128)}, u32[]{:S(2)}) copy-start(f32[768,24]{0,1:T(8,128)} %param.36) | copy-start | bytes 221188
  65.1 414.8 %copy-start.7 = (f32[24,768]{1,0:T(8,128)S(1)}, f32[24,768]{1,0:T(8,128)}, u32[]{:S(2)}) copy-start(f32[24,768]{1,0:T(8,128)} %param.28) | copy-start | bytes 221188
  65.1 414.8 %copy-start.8 = (f32[24,768]{1,0:T(8,128)S(1)}, f32[24,768]{1,0:T(8,128)}, u32[]{:S(2)}) copy-start(f32[24,768]{1,0:T(8,128)} %param.35) | copy-start | bytes 221188
  65.1 415.5 %copy-start.13 = (f32[24,192]{1,0:T(8,128)S(1)}, f32[24,192]{1,0:T(8,128)}, u32[]{:S(2)}) copy-start(f32[24,192]{1,0:T(8,128)} %param.32) | copy-start | bytes 55300
  65.1 415.5 %copy-start.14 = (f32[24,192]{1,0:T(8,128)S(1)}, f32[24,192]{1,0:T(8,128)}, u32[]{:S(2)}) copy-start(f32[24,192]{1,0:T(8,128)} %param.39) | copy-start | bytes 55300
  65.2 415.5 %copy-start.15 = (f32[24,192]{1,0:T(8,128)S(1)}, f32[24,192]{1,0:T(8,128)}, u32[]{:S(2)}) copy-start(f32[24,192]{1,0:T(8,128)} %param.31) | copy-start | bytes 55300
  65.2 415.5 %copy-start.16 = (f32[24,192]{1,0:T(8,128)S(1)}, f32[24,192]{1,0:T(8,128)}, u32[]{:S(2)}) copy-start(f32[24,192]{1,0:T(8,128)} %param.38) | copy-start | bytes 55300
  65.2 493.8 %all-gather.2.cloned.1.call-start = ((), (), s32[]{:S(2)}) async-start(), calls=%async_computation | async-start | bytes 3852288 | tf_op jit(solution)/shard_map/all_gather | solution.py:34
Sparse Core Ops, SparseCore 0:
  65.3 407.5 all-reduce.3
  482.2 76.7 all-gather.1
where the time goes:
time: 578 us; the launch traced here: 577 us
  waiting for transfers between devices  483 us (84%)
  local copies, waits for them, and re-layouts  73.2 us (13%)
  between operations  15 us (3%)
    unnamed x3, waiting for transfers between devices  406 us
    all_gather x1, waiting for transfers between devices, turned_gather(): whole = lax.all_gather(both, axis, axis=0, tiled=True)  76.9 us
    unnamed x59, local copies, waits for them, and re-layouts  21.4 us
    reshape x2, local copies, waits for them, and re-layouts, one_scatter(): lines = jnp.concatenate([b.reshape(devices, -1) for b in blocks], axis=1)  14.5 us
  transfers between devices with their start and end apart: 2, of which 2 were waited for; matrix products, arithmetic and copies ran while one was open for 0% of the time, Pallas kernels for 0%

commit v1 on v0

--- a/solution.py
+++ b/solution.py
@@ -31,7 +31,9 @@
     turned = [jnp.moveaxis(a, dim, 0) for a, dim in zip(arrays, dims)]
     widths = [t[0].size for t in turned]
     both = jnp.concatenate([t.reshape(-1, w) for t, w in zip(turned, widths)], axis=1)
-    whole = lax.all_gather(both, axis, axis=0, tiled=True)
+    whole = jnp.concatenate(
+        lax.all_to_all(jnp.stack([both] * lax.axis_size(axis)), axis, 0, 0), axis=0
+    )
     blocks = jnp.split(whole, [sum(widths[:k]) for k in range(1, len(widths))], axis=1)
     return tuple(
         (

time: 578 us -> 534 us (0.924)
  waiting for transfers between devices: 483 us -> 406 us
  blocking collectives: 0 us -> 37.3 us
    all_gather x1 -> x0, waiting for transfers between devices: 76.9 us -> none  [turned_gather(): whole = lax.all_gather(both, axis, axis=0, tiled=True)]
    all_to_all x0 -> x1, blocking collectives: none -> 37.3 us  [turned_gather(): lax.all_to_all(jnp.stack([both] * lax.axis_size(axis)), axis, 0, 0)]
    unnamed x3 -> x2, waiting for transfers between devices: 406 us -> 406 us
  transfers between devices with their start and end apart: 2 -> 1, of which waited for: 2 -> 1; matrix products, arithmetic and copies ran while one was open for 0% -> 0% of each run, Pallas kernels for 0% -> 0%
where the time goes in v1:
time: 534 us; the launch traced here: 533 us
  waiting for transfers between devices  406 us (76%)
  local copies, waits for them, and re-layouts  69.1 us (13%)
  blocking collectives  37.3 us (7%)
  between operations  15 us (3%)
  other arithmetic  5.58 us (1%)
    unnamed x2, waiting for transfers between devices  406 us
    all_to_all x1, blocking collectives, turned_gather(): lax.all_to_all(jnp.stack([both] * lax.axis_size(axis)), axis, 0, 0)  37.3 us
    unnamed x59, local copies, waits for them, and re-layouts  21.6 us
    reshape x2, local copies, waits for them, and re-layouts, one_scatter(): lines = jnp.concatenate([b.reshape(devices, -1) for b in blocks], axis=1)  14.5 us
  transfers between devices with their start and end apart: 1, of which 1 were waited for; matrix products, arithmetic and copies ran while one was open for 0% of the time, Pallas kernels for 0%

profile of v1, /device:TPU:0, one launch (start us, length us, event | category | flops | bytes accessed | tf_op | source)
XLA Modules:
  0.0 533.1 jit_solution(16932050893258462736)
XLA Ops:
  7.2 2.0 copy.99
  9.3 6.7 %copy.100 = f32[32,768,24]{2,1,0:T(8,128)} copy(f32[32,768,24]{1,2,0:T(8,128)S(1)} %bitcast.23) | data formatting | bytes 4718592 | tf_op jit(solution)/shard_map/transpose | solution.py:13
  16.0 11.5 %reshape.125 = f32[32,18432]{1,0:T(8,128)} reshape(f32[32,768,24]{2,1,0:T(8,128)} %copy.100) | data formatting | bytes 4718592 | tf_op jit(solution)/shard_map/reshape | solution.py:19
  27.5 1.9 reshape_reshape_squeeze.12
  29.4 1.6 constant_dynamic-update-slice_fusion.6
  31.2 1.1 reshape_reshape_squeeze.13
  32.6 1.1 reshape_reshape_squeeze.14
  33.7 1.3 copy.103
  35.0 1.1 reshape_reshape_squeeze.15
  36.1 1.1 copy.104
  37.2 2.0 copy.105
  39.3 3.0 reshape.126
  42.4 3.3 constant_dynamic-update-slice_fusion.5
  45.7 1.9 constant_dynamic-update-slice_fusion.4
  47.6 1.9 constant_dynamic-update-slice_fusion.3
  49.6 0.9 constant_dynamic-update-slice_fusion.2
  50.4 0.9 constant_dynamic-update-slice_fusion.1
  51.9 6.4 %pad.4 = f32[32,56320]{1,0:T(8,128)} pad(f32[32,55320]{1,0:T(8,128)} %constant_dynamic-update-slice_fusion, f32[]{:T(128)} %constant.15.clone.1), padding=0_0x0_1000 | pad | bytes 14289924 | tf_op jit(solution)/shard_map/jit(_pad)/pad | solution.py:21
  58.3 6.8 %reshape.127 = f32[14080,128]{1,0:T(8,128)} reshape(f32[32,56320]{1,0:T(8,128)} %pad.4) | data formatting | bytes 14417920 | tf_op jit(solution)/shard_map/reshape | solution.py:21
  67.0 406.0 %all-reduce.4.cloned.1.call-done = f32[14080,128]{1,0:T(8,128)} async-done(((f32[14080,128]{1,0:T(8,128)}), f32[14080,128]{1,0:T(8,128)}) %all-reduce.4.cloned.1.call-update) | async-done | bytes 7208976
  473.0 0.8 multiply_multiply_fusion.2
  474.7 1.0 multiply_multiply_fusion
  476.4 1.0 dynamic-slice_bitcast_fusion
  479.3 0.7 convert_bitcast_fusion
  481.7 37.3 %all_to_all.5 = bf16[32,24,2305]{2,1,0:T(8,128)(2,1)S(1)} all-to-all(bf16[32,24,2305]{2,1,0:T(8,128)(2,1)S(1)} %stack.2), channel_id=1, replica_groups=mesh['data'=32,'width'=4] {'data'}, dimensions={0} | all-to-all | bytes 7080960 | tf_op jit(solution)/shard_map/all_to_all | solution.py:35
  519.0 1.2 slice_bitcast_fusion
  520.6 0.7 slice_reduce_fusion
  521.3 1.4 copy.111
  522.8 0.9 copy.112
  523.6 0.9 copy.113
  524.5 0.9 copy.114
  525.4 0.9 copy.115
  (75 shorter events, 7.9 us)
Async XLA Ops:
  7.2 465.8 %all-reduce.4.cloned.1.call-start = ((), (), s32[]{:S(2)}) async-start(), calls=%async_computation.1 | async-start | bytes 14417920
  27.5 3.5 copy-start.2
  27.5 4.8 copy-start.3
  31.0 5.1 copy-start.4
  32.3 10.0 %copy-start.17 = (f32[1,768]{1,0:T(1,128)S(1)}, f32[1,768]{1,0:T(1,128)}, u32[]{:S(2)}) copy-start(f32[1,768]{1,0:T(1,128)} %param.27) | copy-start | bytes 9220
  42.3 7.3 %copy-start.1 = (f32[32,4608]{1,0:T(8,128)S(1)}, f32[32,4608]{1,0:T(8,128)}, u32[]{:S(2)}) copy-start(f32[32,4608]{1,0:T(8,128)} %reshape_reshape_squeeze.15) | copy-start | bytes 1769476
  42.3 8.2 %copy-start = (f32[32,4608]{1,0:T(8,128)S(1)}, f32[32,4608]{1,0:T(8,128)}, u32[]{:S(2)}) copy-start(f32[32,4608]{1,0:T(8,128)} %reshape.126) | copy-start | bytes 1769476
  65.1 0.7 copy-start.20
  65.1 412.3 %copy-start.18 = (f32[24]{0:T(128)S(1)}, f32[24]{0:T(128)}, u32[]{:S(2)}) copy-start(f32[24]{0:T(128)} %param.34) | copy-start | bytes 292
  65.1 412.3 %copy-start.19 = (f32[24]{0:T(128)S(1)}, f32[24]{0:T(128)}, u32[]{:S(2)}) copy-start(f32[24]{0:T(128)} %param.41) | copy-start | bytes 292
  65.1 413.0 %copy-start.9 = (f32[192,24]{0,1:T(8,128)S(1)}, f32[192,24]{0,1:T(8,128)}, u32[]{:S(2)}) copy-start(f32[192,24]{0,1:T(8,128)} %param.33) | copy-start | bytes 55300
  65.1 413.0 %copy-start.10 = (f32[192,24]{0,1:T(8,128)S(1)}, f32[192,24]{0,1:T(8,128)}, u32[]{:S(2)}) copy-start(f32[192,24]{0,1:T(8,128)} %param.40) | copy-start | bytes 55300
  65.1 413.6 %copy-start.11 = (f32[24,192]{1,0:T(8,128)S(1)}, f32[24,192]{1,0:T(8,128)}, u32[]{:S(2)}) copy-start(f32[24,192]{1,0:T(8,128)} %param.30) | copy-start | bytes 55300
  65.1 413.6 %copy-start.12 = (f32[24,192]{1,0:T(8,128)S(1)}, f32[24,192]{1,0:T(8,128)}, u32[]{:S(2)}) copy-start(f32[24,192]{1,0:T(8,128)} %param.37) | copy-start | bytes 55300
  65.1 414.2 %copy-start.5 = (f32[768,24]{0,1:T(8,128)S(1)}, f32[768,24]{0,1:T(8,128)}, u32[]{:S(2)}) copy-start(f32[768,24]{0,1:T(8,128)} %param.29) | copy-start | bytes 221188
  65.1 414.2 %copy-start.6 = (f32[768,24]{0,1:T(8,128)S(1)}, f32[768,24]{0,1:T(8,128)}, u32[]{:S(2)}) copy-start(f32[768,24]{0,1:T(8,128)} %param.36) | copy-start | bytes 221188
  65.2 414.8 %copy-start.7 = (f32[24,768]{1,0:T(8,128)S(1)}, f32[24,768]{1,0:T(8,128)}, u32[]{:S(2)}) copy-start(f32[24,768]{1,0:T(8,128)} %param.28) | copy-start | bytes 221188
  65.2 414.8 %copy-start.8 = (f32[24,768]{1,0:T(8,128)S(1)}, f32[24,768]{1,0:T(8,128)}, u32[]{:S(2)}) copy-start(f32[24,768]{1,0:T(8,128)} %param.35) | copy-start | bytes 221188
  65.2 415.5 %copy-start.13 = (f32[24,192]{1,0:T(8,128)S(1)}, f32[24,192]{1,0:T(8,128)}, u32[]{:S(2)}) copy-start(f32[24,192]{1,0:T(8,128)} %param.32) | copy-start | bytes 55300
  65.2 415.5 %copy-start.14 = (f32[24,192]{1,0:T(8,128)S(1)}, f32[24,192]{1,0:T(8,128)}, u32[]{:S(2)}) copy-start(f32[24,192]{1,0:T(8,128)} %param.39) | copy-start | bytes 55300
  65.2 415.5 %copy-start.15 = (f32[24,192]{1,0:T(8,128)S(1)}, f32[24,192]{1,0:T(8,128)}, u32[]{:S(2)}) copy-start(f32[24,192]{1,0:T(8,128)} %param.31) | copy-start | bytes 55300
  65.2 415.5 %copy-start.16 = (f32[24,192]{1,0:T(8,128)S(1)}, f32[24,192]{1,0:T(8,128)}, u32[]{:S(2)}) copy-start(f32[24,192]{1,0:T(8,128)} %param.38) | copy-start | bytes 55300
Sparse Core Ops, SparseCore 0:
  65.4 407.6 all-reduce.3
